TPU v7x, 32 devices: a whole 2x2x4 slice. The times are simulated.
32 devices in a mesh: dev: 8 (over z, y), rep: 4 (over x, core).
Axes of the slice: x: 2, y: 2, z: 4, core: 2. Of those that a mesh axis runs over, the one named last changes fastest.
Arguments:
- features: bfloat16 [32768, 256], P(('dev', 'rep')), may hold values from -6 to 6
- history: bfloat16 [32768, 256], P(('dev', 'rep')), may hold values from -6 to 6
- new_owner: int32 [32, 8], P(('dev', 'rep')), may hold values from 0 to 7, as said below
- pull_rows: int32 [32768], P(('dev', 'rep')), may hold values from 0 to 1023
- occupancy: int32 [256, 16], P(('dev', 'rep')), may hold values from 0 to 1, as said below
- adj_local: bfloat16 [32768, 1024], P(('dev', 'rep')), may hold values from -0.125 to 0.125
- adj_boundary: bfloat16 [32768, 1024], P(('dev', 'rep')), may hold values from -0.125 to 0.125
- w_first: bfloat16 [256, 256], replicated, may hold values from -0.375 to 0.375
- bias_first: float32 [256], replicated, may hold values from -3 to 3
- w_second: bfloat16 [256, 256], replicated, may hold values from -0.375 to 0.375
- cotangent: bfloat16 [32768, 256], P(('dev', 'rep')), may hold values from -6 to 6
Outputs:
- hidden: bfloat16 [32768, 256], P(('dev', 'rep'))
- output: bfloat16 [32768, 256], P(('dev', 'rep'))
- w_second_grad: float32 [256, 256], replicated
Inputs may be any that keep to these rules, and one draw needn't show every extreme that they name: Each row of new_owner is a permutation of 0 to 7. `occupancy`: tile flags of 0 or 1.
All inputs are finite; a program needn't handle non-finite values.
Results may differ from a plain program's by a relative error of at most 0.0061.
Values may be sent and summed in bfloat16 or wider, within the bound.
A program may use at most 64 MiB of HBM per device.

v0:
```python
import jax
import jax.numpy as jnp
from jax import lax
from jax.sharding import PartitionSpec as P


def expand(occupied):
    return jnp.repeat(jnp.repeat(occupied, 128, axis=0), 128, axis=1).astype(jnp.bfloat16)


def dense_terms(owned, remote, adj_local, adj_boundary, occupancy):
    height = owned.shape[0]
    full_mask = expand(occupancy)
    local_tile = adj_local * full_mask[:, :height]
    edge_tile = adj_boundary * full_mask[:, height:]
    summed = jnp.dot(local_tile, owned, preferred_element_type=jnp.float32)
    summed = summed + jnp.dot(edge_tile, remote, preferred_element_type=jnp.float32)
    partial_value = lax.dot_general(
        edge_tile, owned, (((0,), (0,)), ((), ())), preferred_element_type=jnp.float32
    )
    return (summed, partial_value)


def body(
    features,
    history,
    new_owner,
    pull_rows,
    occupancy,
    adj_local,
    adj_boundary,
    w_first,
    bias_first,
    w_second,
    cotangent,
):
    peer_count = lax.axis_size("dev")
    height, breadth = features.shape
    cluster = height // peer_count
    pulled = pull_rows.shape[0]
    per_peer = pulled // peer_count
    indices = jnp.arange(peer_count, dtype=jnp.int32)
    matches = (new_owner[0][:, None] == indices[None, :]).astype(jnp.int32)
    inverse = jnp.sum(matches * indices[:, None], axis=0)

    def arrange(values):
        return values.reshape(peer_count, cluster, breadth)[inverse]

    requests = lax.all_to_all(
        pull_rows.reshape(peer_count, per_peer), "dev", split_axis=0, concat_axis=0, tiled=True
    ).reshape(pulled)

    def fetch_rows(values):
        return values[requests].reshape(peer_count, per_peer, breadth)

    selector = (requests[None, :] == jnp.arange(height, dtype=jnp.int32)[:, None]).astype(
        jnp.bfloat16
    )

    def collect(received):
        return jnp.dot(
            selector, received.reshape(pulled, breadth), preferred_element_type=jnp.float32
        )

    def layer_terms(owned, remote):
        return dense_terms(owned, remote, adj_local, adj_boundary, occupancy)

    moved_x, moved_h = (
        lax.all_to_all(arrange(features), "dev", split_axis=0, concat_axis=0, tiled=True),
        lax.all_to_all(arrange(history), "dev", split_axis=0, concat_axis=0, tiled=True),
    )
    own_x = moved_x.reshape(height, breadth)
    own_h = moved_h.reshape(height, breadth)
    far_x, far_h = (
        lax.all_to_all(fetch_rows(own_x), "dev", split_axis=0, concat_axis=0, tiled=True),
        lax.all_to_all(fetch_rows(own_h), "dev", split_axis=0, concat_axis=0, tiled=True),
    )
    summed_one, partial_one = layer_terms(own_x, far_x.reshape(pulled, breadth))
    pushed_one = lax.all_to_all(
        partial_one.astype(jnp.bfloat16).reshape(peer_count, per_peer, breadth),
        "dev",
        split_axis=0,
        concat_axis=0,
        tiled=True,
    )
    far_h = far_h.reshape(pulled, breadth)
    aggregate_one = (summed_one + collect(pushed_one)).astype(jnp.bfloat16)
    hidden = jnp.maximum(
        jnp.dot(aggregate_one, w_first, preferred_element_type=jnp.float32) + bias_first, 0.0
    ).astype(jnp.bfloat16)
    summed_two, partial_two = layer_terms(hidden, far_h)
    pushed_two = lax.all_to_all(
        partial_two.astype(jnp.bfloat16).reshape(peer_count, per_peer, breadth),
        "dev",
        split_axis=0,
        concat_axis=0,
        tiled=True,
    )
    aggregate_two = (summed_two + collect(pushed_two)).astype(jnp.bfloat16)
    output = jnp.dot(aggregate_two, w_second, preferred_element_type=jnp.float32).astype(
        jnp.bfloat16
    )
    local_grad = lax.dot_general(
        aggregate_two, cotangent, (((0,), (0,)), ((), ())), preferred_element_type=jnp.float32
    )
    gradient = lax.psum(local_grad, ("dev", "rep"))
    return (hidden, output, gradient)


def solution(mesh):
    return jax.shard_map(
        body,
        mesh=mesh,
        in_specs=(
            P(("dev", "rep"), None),
            P(("dev", "rep"), None),
            P(("dev", "rep"), None),
            P(("dev", "rep")),
            P(("dev", "rep"), None),
            P(("dev", "rep"), None),
            P(("dev", "rep"), None),
            P(),
            P(),
            P(),
            P(("dev", "rep"), None),
        ),
        out_specs=(P(("dev", "rep"), None), P(("dev", "rep"), None), P()),
        check_vma=False,
    )
```

profile of v0, /device:TPU:0, one launch (start us, length us, event | category | flops | bytes accessed | tf_op | source)
XLA Modules:
  0.0 263.3 jit_solution(17940252568643423680)
XLA Ops:
  7.2 7.5 %all-to-all-start.1 = ((s32[8,1,128]{2,1,0:T(1,128)}), s32[8,1,128]{2,1,0:T(1,128)S(1)}, u32[]{:S(2)}, u32[]{:S(2)}) async-start(s32[8,1,128]{2,1,0:T(1,128)} %bitcast.62), calls=%async_computation.1 | async-start | bytes 8192 | tf_op jit(solution)/shard_map/all_to_all | solution.py:49
  16.8 4.3 %all-to-all-done.1 = s32[8,1,128]{2,1,0:T(1,128)S(1)} async-done(((s32[8,1,128]{2,1,0:T(1,128)}), s32[8,1,128]{2,1,0:T(1,128)S(1)}, u32[]{:S(2)}, u32[]{:S(2)}) %all-to-all-start.1) | async-done | bytes 4128 | tf_op jit(solution)/shard_map/all_to_all | solution.py:49
  21.1 3.5 %all-to-all-start = ((bf16[8,128,256]{2,1,0:T(8,128)(2,1)}), bf16[8,128,256]{2,1,0:T(8,128)(2,1)S(1)}, u32[]{:S(2)}, u32[]{:S(2)}) async-start(bf16[8,128,256]{2,1,0:T(8,128)(2,1)} %gather_fusion), calls=%async_computation | async-start | bytes 1048576 | tf_op jit(solution)/shard_map/all_to_all | solution.py:69
  25.9 11.9 %all-to-all-done = bf16[8,128,256]{2,1,0:T(8,128)(2,1)S(1)} async-done(((bf16[8,128,256]{2,1,0:T(8,128)(2,1)}), bf16[8,128,256]{2,1,0:T(8,128)(2,1)S(1)}, u32[]{:S(2)}, u32[]{:S(2)}) %all-to-all-start) | async-done | bytes 524320 | tf_op jit(solution)/shard_map/all_to_all | solution.py:69
  37.8 3.7 %all-to-all-start.4 = ((bf16[8,128,256]{2,1,0:T(8,128)(2,1)}), bf16[8,128,256]{2,1,0:T(8,128)(2,1)S(1)}, u32[]{:S(2)}, u32[]{:S(2)}) async-start(bf16[8,128,256]{2,1,0:T(8,128)(2,1)} %gather_fusion.2), calls=%async_computation.4 | async-start | bytes 1048576 | tf_op jit(solution)/shard_map/all_to_all | solution.py:70
  41.5 5.0 %gather_fusion.1 = bf16[1024,256]{1,0:T(8,128)(2,1)} fusion(bf16[1024,256]{1,0:T(8,128)(2,1)S(1)} %bitcast.45, s32[1024]{0:T(1024)S(1)} %broadcast_clamp_fusion), kind=kCustom, calls=%fused_computation.1 | custom fusion | bytes 1052672 | tf_op jit(solution)/shard_map/gather | solution.py:54
  46.5 8.8 %all-to-all-done.4 = bf16[8,128,256]{2,1,0:T(8,128)(2,1)S(1)} async-done(((bf16[8,128,256]{2,1,0:T(8,128)(2,1)}), bf16[8,128,256]{2,1,0:T(8,128)(2,1)S(1)}, u32[]{:S(2)}, u32[]{:S(2)}) %all-to-all-start.4) | async-done | bytes 524320 | tf_op jit(solution)/shard_map/all_to_all | solution.py:70
  55.3 4.2 %all-to-all-start.2 = ((bf16[8,128,256]{2,1,0:T(8,128)(2,1)}), bf16[8,128,256]{2,1,0:T(8,128)(2,1)}, u32[]{:S(2)}, u32[]{:S(2)}) async-start(bf16[8,128,256]{2,1,0:T(8,128)(2,1)} %bitcast.9), calls=%async_computation.2 | async-start | bytes 1048576 | tf_op jit(solution)/shard_map/all_to_all | solution.py:75
  59.5 4.5 %broadcast_in_dim.5 = bf16[1024,16,128]{2,1,0:T(8,128)(2,1)S(1)} broadcast(bf16[1024,16]{1,0:T(8,128)(2,1)S(1)} %bitcast.55), dimensions={0,1} | broadcast | bytes 4227072 | tf_op jit(solution)/shard_map/broadcast_in_dim | solution.py:8
  69.7 3.5 %all-to-all-done.2 = bf16[8,128,256]{2,1,0:T(8,128)(2,1)} async-done(((bf16[8,128,256]{2,1,0:T(8,128)(2,1)}), bf16[8,128,256]{2,1,0:T(8,128)(2,1)}, u32[]{:S(2)}, u32[]{:S(2)}) %all-to-all-start.2) | async-done | bytes 524320 | tf_op jit(solution)/shard_map/all_to_all | solution.py:75
  73.2 4.1 %all-to-all-start.3 = ((bf16[8,128,256]{2,1,0:T(8,128)(2,1)}), bf16[8,128,256]{2,1,0:T(8,128)(2,1)}, u32[]{:S(2)}, u32[]{:S(2)}) async-start(bf16[8,128,256]{2,1,0:T(8,128)(2,1)} %bitcast.57), calls=%async_computation.3 | async-start | bytes 1048576 | tf_op jit(solution)/shard_map/all_to_all | solution.py:79
  77.4 5.7 %gather_fusion.3 = bf16[1024,256]{1,0:T(8,128)(2,1)} fusion(bf16[1024,256]{1,0:T(8,128)(2,1)} %bitcast.48, s32[1024]{0:T(1024)S(1)} %broadcast_clamp_fusion), kind=kCustom, calls=%fused_computation.3 | custom fusion | bytes 1052672 | tf_op jit(solution)/shard_map/gather | solution.py:54
  83.1 3.9 %fusion.11 = f32[1024,256]{1,0:T(8,128)} fusion(bf16[1024,256]{1,0:T(8,128)(2,1)S(1)} %bitcast.47, bf16[1024,1024]{1,0:T(8,128)(2,1)} %param.16, bf16[1024,2048]{1,0:T(8,128)(2,1)} %bitcast.51), kind=kOutput, calls=%fused_computation.25 | convolution fusion | flops 537919488 | bytes 5767168 | tf_op jit(solution)/shard_map/dot_general | solution.py:16
  87.0 3.7 %all-to-all-done.3 = bf16[8,128,256]{2,1,0:T(8,128)(2,1)} async-done(((bf16[8,128,256]{2,1,0:T(8,128)(2,1)}), bf16[8,128,256]{2,1,0:T(8,128)(2,1)}, u32[]{:S(2)}, u32[]{:S(2)}) %all-to-all-start.3) | async-done | bytes 524320 | tf_op jit(solution)/shard_map/all_to_all | solution.py:79
  90.7 3.7 %all-to-all-start.5 = ((bf16[8,128,256]{2,1,0:T(8,128)(2,1)}), bf16[8,128,256]{2,1,0:T(8,128)(2,1)S(1)}, u32[]{:S(2)}, u32[]{:S(2)}) async-start(bf16[8,128,256]{2,1,0:T(8,128)(2,1)} %bitcast.53), calls=%async_computation.5 | async-start | bytes 1048576 | tf_op jit(solution)/shard_map/all_to_all | solution.py:76
  94.4 3.1 %convolution_add_fusion.2 = f32[1024,256]{1,0:T(8,128)} fusion(f32[1024,256]{1,0:T(8,128)} %fusion.11, bf16[1024,1024]{1,0:T(8,128)(2,1)S(1)} %slice_multiply_fusion, bf16[1024,256]{1,0:T(8,128)(2,1)} %bitcast.10), kind=kOutput, calls=%fused_computation.17 | convolution fusion | flops 537133056 | bytes 4718592 | tf_op jit(solution)/shard_map/dot_general | solution.py:17
  97.5 3.2 %fusion.7 = bf16[1024,256]{1,0:T(8,128)(2,1)} fusion(bf16[256,256]{1,0:T(8,128)(2,1)S(1)} %copy-done.8, f32[1024,256]{1,0:T(8,128)} %convolution_add_fusion.2, bf16[1024,256]{1,0:T(8,128)(2,1)} %bitcast.13, s32[1024]{0:T(1024)S(1)} %bitcast.59, f32[256]{0:T(256)S(1)} %copy-done.9), kind=kOutput, calls=%fused_computation.18 | convolution fusion | flops 673447936 | bytes 2233344 | tf_op jit(solution)/shard_map/dot_general | solution.py:89
  100.7 2.6 convolution_convert_fusion.1
  103.3 4.8 %all-to-all-done.5 = bf16[8,128,256]{2,1,0:T(8,128)(2,1)S(1)} async-done(((bf16[8,128,256]{2,1,0:T(8,128)(2,1)}), bf16[8,128,256]{2,1,0:T(8,128)(2,1)S(1)}, u32[]{:S(2)}, u32[]{:S(2)}) %all-to-all-start.5) | async-done | bytes 524320 | tf_op jit(solution)/shard_map/all_to_all | solution.py:76
  108.2 4.1 %all-to-all-start.6 = ((bf16[8,128,256]{2,1,0:T(8,128)(2,1)}), bf16[8,128,256]{2,1,0:T(8,128)(2,1)}, u32[]{:S(2)}, u32[]{:S(2)}) async-start(bf16[8,128,256]{2,1,0:T(8,128)(2,1)} %bitcast.56), calls=%async_computation.6 | async-start | bytes 1048576 | tf_op jit(solution)/shard_map/all_to_all | solution.py:92
  112.5 3.0 %fusion.10 = f32[1024,256]{1,0:T(8,128)S(1)} fusion(bf16[1024,256]{1,0:T(8,128)(2,1)} %fusion.7, bf16[1024,1024]{1,0:T(8,128)(2,1)} %param.16, bf16[1024,2048]{1,0:T(8,128)(2,1)} %bitcast.52), kind=kOutput, calls=%fused_computation.24 | convolution fusion | flops 537919488 | bytes 5767168 | tf_op jit(solution)/shard_map/dot_general | solution.py:16
  117.3 8.4 %all-to-all-done.6 = bf16[8,128,256]{2,1,0:T(8,128)(2,1)} async-done(((bf16[8,128,256]{2,1,0:T(8,128)(2,1)}), bf16[8,128,256]{2,1,0:T(8,128)(2,1)}, u32[]{:S(2)}, u32[]{:S(2)}) %all-to-all-start.6) | async-done | bytes 524320 | tf_op jit(solution)/shard_map/all_to_all | solution.py:92
  125.7 2.2 fusion.8
  130.1 124.7 %all-reduce.2.cloned.1.call-done = f32[256,256]{1,0:T(8,128)} async-done(((f32[256,256]{1,0:T(8,128)}), f32[256,256]{1,0:T(8,128)}) %all-reduce.2.cloned.1.call-update) | async-done | bytes 262160 | tf_op jit(solution)/shard_map/psum | solution.py:106
  (38 shorter events, 15.0 us)
Async XLA Ops:
  7.2 8.2 %copy-start = (bf16[1024,256]{1,0:T(8,128)(2,1)S(1)}, bf16[1024,256]{1,0:T(8,128)(2,1)}, u32[]{:S(2)}) copy-start(bf16[1024,256]{1,0:T(8,128)(2,1)} %param.11) | copy-start | bytes 1572868
  7.2 17.4 %copy-start.5 = (bf16[1024,256]{1,0:T(8,128)(2,1)S(1)}, bf16[1024,256]{1,0:T(8,128)(2,1)}, u32[]{:S(2)}) copy-start(bf16[1024,256]{1,0:T(8,128)(2,1)} %param.12) | copy-start | bytes 1572868
  7.2 13.9 %all-to-all-start.1 = ((s32[8,1,128]{2,1,0:T(1,128)}), s32[8,1,128]{2,1,0:T(1,128)S(1)}, u32[]{:S(2)}, u32[]{:S(2)}) async-start(s32[8,1,128]{2,1,0:T(1,128)} %bitcast.62), calls=%async_computation.1 | async-start | bytes 8192 | tf_op jit(solution)/shard_map/all_to_all | solution.py:49
  21.1 16.8 %all-to-all-start = ((bf16[8,128,256]{2,1,0:T(8,128)(2,1)}), bf16[8,128,256]{2,1,0:T(8,128)(2,1)S(1)}, u32[]{:S(2)}, u32[]{:S(2)}) async-start(bf16[8,128,256]{2,1,0:T(8,128)(2,1)} %gather_fusion), calls=%async_computation | async-start | bytes 1048576 | tf_op jit(solution)/shard_map/all_to_all | solution.py:69
  37.8 17.5 %all-to-all-start.4 = ((bf16[8,128,256]{2,1,0:T(8,128)(2,1)}), bf16[8,128,256]{2,1,0:T(8,128)(2,1)S(1)}, u32[]{:S(2)}, u32[]{:S(2)}) async-start(bf16[8,128,256]{2,1,0:T(8,128)(2,1)} %gather_fusion.2), calls=%async_computation.4 | async-start | bytes 1048576 | tf_op jit(solution)/shard_map/all_to_all | solution.py:70
  41.5 18.0 %copy-start.7 = (s32[8,16]{1,0:T(8,128)S(1)}, s32[8,16]{1,0:T(8,128)}, u32[]{:S(2)}) copy-start(s32[8,16]{1,0:T(8,128)} %param.15) | copy-start | bytes 1540
  55.3 8.7 %copy-start.1 = (bf16[8,128,256]{2,1,0:T(8,128)(2,1)}, bf16[8,128,256]{2,1,0:T(8,128)(2,1)S(1)}, u32[]{:S(2)}) copy-start(bf16[8,128,256]{2,1,0:T(8,128)(2,1)S(1)} %all-to-all-done.4) | copy-start | bytes 1572868
  55.3 17.9 %all-to-all-start.2 = ((bf16[8,128,256]{2,1,0:T(8,128)(2,1)}), bf16[8,128,256]{2,1,0:T(8,128)(2,1)}, u32[]{:S(2)}, u32[]{:S(2)}) async-start(bf16[8,128,256]{2,1,0:T(8,128)(2,1)} %bitcast.9), calls=%async_computation.2 | async-start | bytes 1048576 | tf_op jit(solution)/shard_map/all_to_all | solution.py:75
  64.0 2.2 copy-start.3
  66.2 1.9 copy-start.2
  73.2 17.5 %all-to-all-start.3 = ((bf16[8,128,256]{2,1,0:T(8,128)(2,1)}), bf16[8,128,256]{2,1,0:T(8,128)(2,1)}, u32[]{:S(2)}, u32[]{:S(2)}) async-start(bf16[8,128,256]{2,1,0:T(8,128)(2,1)} %bitcast.57), calls=%async_computation.3 | async-start | bytes 1048576 | tf_op jit(solution)/shard_map/all_to_all | solution.py:79
  90.7 17.5 %all-to-all-start.5 = ((bf16[8,128,256]{2,1,0:T(8,128)(2,1)}), bf16[8,128,256]{2,1,0:T(8,128)(2,1)S(1)}, u32[]{:S(2)}, u32[]{:S(2)}) async-start(bf16[8,128,256]{2,1,0:T(8,128)(2,1)} %bitcast.53), calls=%async_computation.5 | async-start | bytes 1048576 | tf_op jit(solution)/shard_map/all_to_all | solution.py:76
  94.4 3.1 %copy-start.8 = (bf16[256,256]{1,0:T(8,128)(2,1)S(1)}, bf16[256,256]{1,0:T(8,128)(2,1)}, u32[]{:S(2)}) copy-start(bf16[256,256]{1,0:T(8,128)(2,1)} %param.18) | copy-start | bytes 393220
  94.4 3.1 %copy-start.9 = (f32[256]{0:T(256)S(1)}, f32[256]{0:T(256)}, u32[]{:S(2)}) copy-start(f32[256]{0:T(256)} %param.19) | copy-start | bytes 3076
  108.2 17.5 %all-to-all-start.6 = ((bf16[8,128,256]{2,1,0:T(8,128)(2,1)}), bf16[8,128,256]{2,1,0:T(8,128)(2,1)}, u32[]{:S(2)}, u32[]{:S(2)}) async-start(bf16[8,128,256]{2,1,0:T(8,128)(2,1)} %bitcast.56), calls=%async_computation.6 | async-start | bytes 1048576 | tf_op jit(solution)/shard_map/all_to_all | solution.py:92
  112.3 142.5 %all-reduce.2.cloned.1.call-start = ((), (), s32[]{:S(2)}) async-start(), calls=%async_computation.7 | async-start | bytes 524288 | tf_op jit(solution)/shard_map/psum | solution.py:106
  117.3 10.7 %copy-start.4 = (bf16[1024,256]{1,0:T(8,128)(2,1)S(1)}, bf16[1024,256]{1,0:T(8,128)(2,1)}, u32[]{:S(2)}) copy-start(bf16[1024,256]{1,0:T(8,128)(2,1)} %param.21) | copy-start | bytes 1572868
  125.7 3.3 %copy-start.6 = (bf16[256,256]{1,0:T(8,128)(2,1)S(1)}, bf16[256,256]{1,0:T(8,128)(2,1)}, u32[]{:S(2)}) copy-start(bf16[256,256]{1,0:T(8,128)(2,1)} %param.20) | copy-start | bytes 393220
Sparse Core Ops, SparseCore 0:
  129.1 125.6 all-reduce.1
where the time goes:
time: 264 us; the launch traced here: 263 us
  waiting for transfers between devices  170 us (64%)
  starting transfers between devices  31 us (12%)
  local copies, waits for them, and re-layouts  23.5 us (9%)
  matrix products  23.5 us (9%)
  between operations  14.2 us (5%)
    psum x1, waiting for transfers between devices, body(): gradient = lax.psum(local_grad, ('dev', 'rep'))  125 us
    all_to_all x1, waiting for transfers between devices, body(): lax.all_to_all(arrange(features), 'dev', split_axis=0, concat_axis=0, til...  11.9 us
    gather x2, local copies, waits for them, and re-layouts, fetch_rows(): return values[requests].reshape(peer_count, per_peer, breadth)  10.7 us
    all_to_all x1, waiting for transfers between devices, body(): lax.all_to_all(arrange(history), 'dev', split_axis=0, concat_axis=0, tile...  8.81 us
    all_to_all x1, waiting for transfers between devices, body(): lax.all_to_all(partial_two.astype(jnp.bfloat16).reshape(peer_count, per_p...  8.41 us
    all_to_all x1, starting transfers between devices, body(): lax.all_to_all(pull_rows.reshape(peer_count, per_peer), 'dev', split_axis...  7.45 us
    dot_general x2, matrix products, dense_terms(): summed = jnp.dot(local_tile, owned, preferred_element_type=jnp.float32)  6.92 us
    unnamed x22, local copies, waits for them, and re-layouts  5.58 us
  transfers between devices with their start and end apart: 8, of which 8 were waited for; matrix products, arithmetic and copies ran while one was open for 16% of the time, Pallas kernels for 0%

commit v1 on v0

--- a/solution.py
+++ b/solution.py
@@ -103,7 +103,7 @@
     local_grad = lax.dot_general(
         aggregate_two, cotangent, (((0,), (0,)), ((), ())), preferred_element_type=jnp.float32
     )
-    gradient = lax.psum(local_grad, ("dev", "rep"))
+    gradient = lax.psum(lax.psum(local_grad, "rep"), "dev")
     return (hidden, output, gradient)
 
 

time: 264 us -> 244 us (0.924)
  waiting for transfers between devices: 170 us -> 150 us
    psum x1 -> x2, waiting for transfers between devices: 125 us -> 105 us  [body(): gradient = lax.psum(lax.psum(local_grad, 'rep'), 'dev')]
  transfers between devices with their start and end apart: 8 -> 9, of which waited for: 8 -> 9; matrix products, arithmetic and copies ran while one was open for 16% -> 17% of each run, Pallas kernels for 0% -> 0%
where the time goes in v1:
time: 244 us; the launch traced here: 243 us
  waiting for transfers between devices  150 us (61%)
  starting transfers between devices  30.8 us (13%)
  local copies, waits for them, and re-layouts  23.5 us (10%)
  matrix products  23.5 us (10%)
  between operations  14.2 us (6%)
    psum x2, waiting for transfers between devices, body(): gradient = lax.psum(lax.psum(local_grad, 'rep'), 'dev')  105 us
    all_to_all x1, waiting for transfers between devices, body(): lax.all_to_all(arrange(features), 'dev', split_axis=0, concat_axis=0, til...  11.9 us
    gather x2, local copies, waits for them, and re-layouts, fetch_rows(): return values[requests].reshape(peer_count, per_peer, breadth)  10.7 us
    all_to_all x1, waiting for transfers between devices, body(): lax.all_to_all(arrange(history), 'dev', split_axis=0, concat_axis=0, tile...  8.81 us
    all_to_all x1, waiting for transfers between devices, body(): lax.all_to_all(partial_two.astype(jnp.bfloat16).reshape(peer_count, per_p...  8.59 us
    all_to_all x1, starting transfers between devices, body(): lax.all_to_all(pull_rows.reshape(peer_count, per_peer), 'dev', split_axis...  7.45 us
    dot_general x2, matrix products, dense_terms(): summed = jnp.dot(local_tile, owned, preferred_element_type=jnp.float32)  6.91 us
    unnamed x22, local copies, waits for them, and re-layouts  5.58 us
  transfers between devices with their start and end apart: 9, of which 9 were waited for; matrix products, arithmetic and copies ran while one was open for 17% of the time, Pallas kernels for 0%

profile of v1, /device:TPU:0, one launch (start us, length us, event | category | flops | bytes accessed | tf_op | source)
XLA Modules:
  0.0 243.5 jit_solution(10179461771275953720)
XLA Ops:
  7.2 7.5 %all-to-all-start.1 = ((s32[8,1,128]{2,1,0:T(1,128)}), s32[8,1,128]{2,1,0:T(1,128)S(1)}, u32[]{:S(2)}, u32[]{:S(2)}) async-start(s32[8,1,128]{2,1,0:T(1,128)} %bitcast.62), calls=%async_computation.1 | async-start | bytes 8192 | tf_op jit(solution)/shard_map/all_to_all | solution.py:49
  16.8 4.3 %all-to-all-done.1 = s32[8,1,128]{2,1,0:T(1,128)S(1)} async-done(((s32[8,1,128]{2,1,0:T(1,128)}), s32[8,1,128]{2,1,0:T(1,128)S(1)}, u32[]{:S(2)}, u32[]{:S(2)}) %all-to-all-start.1) | async-done | bytes 4128 | tf_op jit(solution)/shard_map/all_to_all | solution.py:49
  21.1 3.5 %all-to-all-start = ((bf16[8,128,256]{2,1,0:T(8,128)(2,1)}), bf16[8,128,256]{2,1,0:T(8,128)(2,1)S(1)}, u32[]{:S(2)}, u32[]{:S(2)}) async-start(bf16[8,128,256]{2,1,0:T(8,128)(2,1)} %gather_fusion), calls=%async_computation | async-start | bytes 1048576 | tf_op jit(solution)/shard_map/all_to_all | solution.py:69
  25.9 11.9 %all-to-all-done = bf16[8,128,256]{2,1,0:T(8,128)(2,1)S(1)} async-done(((bf16[8,128,256]{2,1,0:T(8,128)(2,1)}), bf16[8,128,256]{2,1,0:T(8,128)(2,1)S(1)}, u32[]{:S(2)}, u32[]{:S(2)}) %all-to-all-start) | async-done | bytes 524320 | tf_op jit(solution)/shard_map/all_to_all | solution.py:69
  37.8 3.7 %all-to-all-start.4 = ((bf16[8,128,256]{2,1,0:T(8,128)(2,1)}), bf16[8,128,256]{2,1,0:T(8,128)(2,1)S(1)}, u32[]{:S(2)}, u32[]{:S(2)}) async-start(bf16[8,128,256]{2,1,0:T(8,128)(2,1)} %gather_fusion.2), calls=%async_computation.4 | async-start | bytes 1048576 | tf_op jit(solution)/shard_map/all_to_all | solution.py:70
  41.5 5.0 %gather_fusion.1 = bf16[1024,256]{1,0:T(8,128)(2,1)} fusion(bf16[1024,256]{1,0:T(8,128)(2,1)S(1)} %bitcast.45, s32[1024]{0:T(1024)S(1)} %broadcast_clamp_fusion), kind=kCustom, calls=%fused_computation.1 | custom fusion | bytes 1052672 | tf_op jit(solution)/shard_map/gather | solution.py:54
  46.5 8.8 %all-to-all-done.4 = bf16[8,128,256]{2,1,0:T(8,128)(2,1)S(1)} async-done(((bf16[8,128,256]{2,1,0:T(8,128)(2,1)}), bf16[8,128,256]{2,1,0:T(8,128)(2,1)S(1)}, u32[]{:S(2)}, u32[]{:S(2)}) %all-to-all-start.4) | async-done | bytes 524320 | tf_op jit(solution)/shard_map/all_to_all | solution.py:70
  55.3 4.2 %all-to-all-start.2 = ((bf16[8,128,256]{2,1,0:T(8,128)(2,1)}), bf16[8,128,256]{2,1,0:T(8,128)(2,1)}, u32[]{:S(2)}, u32[]{:S(2)}) async-start(bf16[8,128,256]{2,1,0:T(8,128)(2,1)} %bitcast.9), calls=%async_computation.2 | async-start | bytes 1048576 | tf_op jit(solution)/shard_map/all_to_all | solution.py:75
  59.5 4.5 %broadcast_in_dim.5 = bf16[1024,16,128]{2,1,0:T(8,128)(2,1)S(1)} broadcast(bf16[1024,16]{1,0:T(8,128)(2,1)S(1)} %bitcast.55), dimensions={0,1} | broadcast | bytes 4227072 | tf_op jit(solution)/shard_map/broadcast_in_dim | solution.py:8
  69.7 3.5 %all-to-all-done.2 = bf16[8,128,256]{2,1,0:T(8,128)(2,1)} async-done(((bf16[8,128,256]{2,1,0:T(8,128)(2,1)}), bf16[8,128,256]{2,1,0:T(8,128)(2,1)}, u32[]{:S(2)}, u32[]{:S(2)}) %all-to-all-start.2) | async-done | bytes 524320 | tf_op jit(solution)/shard_map/all_to_all | solution.py:75
  73.2 4.1 %all-to-all-start.3 = ((bf16[8,128,256]{2,1,0:T(8,128)(2,1)}), bf16[8,128,256]{2,1,0:T(8,128)(2,1)}, u32[]{:S(2)}, u32[]{:S(2)}) async-start(bf16[8,128,256]{2,1,0:T(8,128)(2,1)} %bitcast.57), calls=%async_computation.3 | async-start | bytes 1048576 | tf_op jit(solution)/shard_map/all_to_all | solution.py:79
  77.4 5.7 %gather_fusion.3 = bf16[1024,256]{1,0:T(8,128)(2,1)} fusion(bf16[1024,256]{1,0:T(8,128)(2,1)} %bitcast.48, s32[1024]{0:T(1024)S(1)} %broadcast_clamp_fusion), kind=kCustom, calls=%fused_computation.3 | custom fusion | bytes 1052672 | tf_op jit(solution)/shard_map/gather | solution.py:54
  83.1 3.9 %fusion.11 = f32[1024,256]{1,0:T(8,128)} fusion(bf16[1024,256]{1,0:T(8,128)(2,1)S(1)} %bitcast.47, bf16[1024,1024]{1,0:T(8,128)(2,1)} %param.16, bf16[1024,2048]{1,0:T(8,128)(2,1)} %bitcast.51), kind=kOutput, calls=%fused_computation.25 | convolution fusion | flops 537919488 | bytes 5767168 | tf_op jit(solution)/shard_map/dot_general | solution.py:16
  87.0 3.7 %all-to-all-done.3 = bf16[8,128,256]{2,1,0:T(8,128)(2,1)} async-done(((bf16[8,128,256]{2,1,0:T(8,128)(2,1)}), bf16[8,128,256]{2,1,0:T(8,128)(2,1)}, u32[]{:S(2)}, u32[]{:S(2)}) %all-to-all-start.3) | async-done | bytes 524320 | tf_op jit(solution)/shard_map/all_to_all | solution.py:79
  90.7 3.7 %all-to-all-start.5 = ((bf16[8,128,256]{2,1,0:T(8,128)(2,1)}), bf16[8,128,256]{2,1,0:T(8,128)(2,1)S(1)}, u32[]{:S(2)}, u32[]{:S(2)}) async-start(bf16[8,128,256]{2,1,0:T(8,128)(2,1)} %bitcast.53), calls=%async_computation.5 | async-start | bytes 1048576 | tf_op jit(solution)/shard_map/all_to_all | solution.py:76
  94.4 3.1 %convolution_add_fusion.2 = f32[1024,256]{1,0:T(8,128)} fusion(f32[1024,256]{1,0:T(8,128)} %fusion.11, bf16[1024,1024]{1,0:T(8,128)(2,1)S(1)} %slice_multiply_fusion, bf16[1024,256]{1,0:T(8,128)(2,1)} %bitcast.10), kind=kOutput, calls=%fused_computation.17 | convolution fusion | flops 537133056 | bytes 4718592 | tf_op jit(solution)/shard_map/dot_general | solution.py:17
  97.5 3.2 %fusion.7 = bf16[1024,256]{1,0:T(8,128)(2,1)} fusion(bf16[256,256]{1,0:T(8,128)(2,1)S(1)} %copy-done.8, f32[1024,256]{1,0:T(8,128)} %convolution_add_fusion.2, bf16[1024,256]{1,0:T(8,128)(2,1)} %bitcast.13, s32[1024]{0:T(1024)S(1)} %bitcast.59, f32[256]{0:T(256)S(1)} %copy-done.9), kind=kOutput, calls=%fused_computation.18 | convolution fusion | flops 673447936 | bytes 2233344 | tf_op jit(solution)/shard_map/dot_general | solution.py:89
  100.7 2.6 %convolution_convert_fusion.1 = bf16[1024,256]{1,0:T(8,128)(2,1)} fusion(bf16[1024,1024]{1,0:T(8,128)(2,1)S(1)} %slice_multiply_fusion, bf16[1024,256]{1,0:T(8,128)(2,1)} %fusion.7), kind=kOutput, calls=%fused_computation.22 | convolution fusion | flops 537133056 | bytes 3145728 | tf_op jit(solution)/shard_map/dot_general | solution.py:18
  103.3 4.8 %all-to-all-done.5 = bf16[8,128,256]{2,1,0:T(8,128)(2,1)S(1)} async-done(((bf16[8,128,256]{2,1,0:T(8,128)(2,1)}), bf16[8,128,256]{2,1,0:T(8,128)(2,1)S(1)}, u32[]{:S(2)}, u32[]{:S(2)}) %all-to-all-start.5) | async-done | bytes 524320 | tf_op jit(solution)/shard_map/all_to_all | solution.py:76
  108.2 4.1 %all-to-all-start.6 = ((bf16[8,128,256]{2,1,0:T(8,128)(2,1)}), bf16[8,128,256]{2,1,0:T(8,128)(2,1)}, u32[]{:S(2)}, u32[]{:S(2)}) async-start(bf16[8,128,256]{2,1,0:T(8,128)(2,1)} %bitcast.56), calls=%async_computation.6 | async-start | bytes 1048576 | tf_op jit(solution)/shard_map/all_to_all | solution.py:92
  112.4 3.0 %fusion.10 = f32[1024,256]{1,0:T(8,128)S(1)} fusion(bf16[1024,256]{1,0:T(8,128)(2,1)} %fusion.7, bf16[1024,1024]{1,0:T(8,128)(2,1)} %param.16, bf16[1024,2048]{1,0:T(8,128)(2,1)} %bitcast.52), kind=kOutput, calls=%fused_computation.24 | convolution fusion | flops 537919488 | bytes 5767168 | tf_op jit(solution)/shard_map/dot_general | solution.py:16
  117.1 8.6 %all-to-all-done.6 = bf16[8,128,256]{2,1,0:T(8,128)(2,1)} async-done(((bf16[8,128,256]{2,1,0:T(8,128)(2,1)}), bf16[8,128,256]{2,1,0:T(8,128)(2,1)}, u32[]{:S(2)}, u32[]{:S(2)}) %all-to-all-start.6) | async-done | bytes 524320 | tf_op jit(solution)/shard_map/all_to_all | solution.py:92
  129.1 31.5 %all-reduce.3.cloned.1.call-done = f32[256,256]{1,0:T(8,128)} async-done(((f32[256,256]{1,0:T(8,128)}), f32[256,256]{1,0:T(8,128)}) %all-reduce.3.cloned.1.call-update) | async-done | bytes 262160 | tf_op jit(solution)/shard_map/psum | solution.py:106
  161.7 73.3 %all-reduce.5.cloned.1.call-done = f32[256,256]{1,0:T(8,128)} async-done(((f32[256,256]{1,0:T(8,128)}), f32[256,256]{1,0:T(8,128)}) %all-reduce.5.cloned.1.call-update) | async-done | bytes 262160 | tf_op jit(solution)/shard_map/psum | solution.py:106
  (41 shorter events, 17.1 us)
Async XLA Ops:
  7.2 8.2 %copy-start = (bf16[1024,256]{1,0:T(8,128)(2,1)S(1)}, bf16[1024,256]{1,0:T(8,128)(2,1)}, u32[]{:S(2)}) copy-start(bf16[1024,256]{1,0:T(8,128)(2,1)} %param.11) | copy-start | bytes 1572868
  7.2 17.4 %copy-start.5 = (bf16[1024,256]{1,0:T(8,128)(2,1)S(1)}, bf16[1024,256]{1,0:T(8,128)(2,1)}, u32[]{:S(2)}) copy-start(bf16[1024,256]{1,0:T(8,128)(2,1)} %param.12) | copy-start | bytes 1572868
  7.2 13.9 %all-to-all-start.1 = ((s32[8,1,128]{2,1,0:T(1,128)}), s32[8,1,128]{2,1,0:T(1,128)S(1)}, u32[]{:S(2)}, u32[]{:S(2)}) async-start(s32[8,1,128]{2,1,0:T(1,128)} %bitcast.62), calls=%async_computation.1 | async-start | bytes 8192 | tf_op jit(solution)/shard_map/all_to_all | solution.py:49
  21.1 16.8 %all-to-all-start = ((bf16[8,128,256]{2,1,0:T(8,128)(2,1)}), bf16[8,128,256]{2,1,0:T(8,128)(2,1)S(1)}, u32[]{:S(2)}, u32[]{:S(2)}) async-start(bf16[8,128,256]{2,1,0:T(8,128)(2,1)} %gather_fusion), calls=%async_computation | async-start | bytes 1048576 | tf_op jit(solution)/shard_map/all_to_all | solution.py:69
  37.8 17.5 %all-to-all-start.4 = ((bf16[8,128,256]{2,1,0:T(8,128)(2,1)}), bf16[8,128,256]{2,1,0:T(8,128)(2,1)S(1)}, u32[]{:S(2)}, u32[]{:S(2)}) async-start(bf16[8,128,256]{2,1,0:T(8,128)(2,1)} %gather_fusion.2), calls=%async_computation.4 | async-start | bytes 1048576 | tf_op jit(solution)/shard_map/all_to_all | solution.py:70
  41.5 18.0 %copy-start.7 = (s32[8,16]{1,0:T(8,128)S(1)}, s32[8,16]{1,0:T(8,128)}, u32[]{:S(2)}) copy-start(s32[8,16]{1,0:T(8,128)} %param.15) | copy-start | bytes 1540
  55.3 8.7 %copy-start.1 = (bf16[8,128,256]{2,1,0:T(8,128)(2,1)}, bf16[8,128,256]{2,1,0:T(8,128)(2,1)S(1)}, u32[]{:S(2)}) copy-start(bf16[8,128,256]{2,1,0:T(8,128)(2,1)S(1)} %all-to-all-done.4) | copy-start | bytes 1572868
  55.3 17.9 %all-to-all-start.2 = ((bf16[8,128,256]{2,1,0:T(8,128)(2,1)}), bf16[8,128,256]{2,1,0:T(8,128)(2,1)}, u32[]{:S(2)}, u32[]{:S(2)}) async-start(bf16[8,128,256]{2,1,0:T(8,128)(2,1)} %bitcast.9), calls=%async_computation.2 | async-start | bytes 1048576 | tf_op jit(solution)/shard_map/all_to_all | solution.py:75
  64.0 2.2 copy-start.3
  66.2 1.9 copy-start.2
  73.2 17.5 %all-to-all-start.3 = ((bf16[8,128,256]{2,1,0:T(8,128)(2,1)}), bf16[8,128,256]{2,1,0:T(8,128)(2,1)}, u32[]{:S(2)}, u32[]{:S(2)}) async-start(bf16[8,128,256]{2,1,0:T(8,128)(2,1)} %bitcast.57), calls=%async_computation.3 | async-start | bytes 1048576 | tf_op jit(solution)/shard_map/all_to_all | solution.py:79
  90.7 17.5 %all-to-all-start.5 = ((bf16[8,128,256]{2,1,0:T(8,128)(2,1)}), bf16[8,128,256]{2,1,0:T(8,128)(2,1)S(1)}, u32[]{:S(2)}, u32[]{:S(2)}) async-start(bf16[8,128,256]{2,1,0:T(8,128)(2,1)} %bitcast.53), calls=%async_computation.5 | async-start | bytes 1048576 | tf_op jit(solution)/shard_map/all_to_all | solution.py:76
  94.4 3.1 %copy-start.8 = (bf16[256,256]{1,0:T(8,128)(2,1)S(1)}, bf16[256,256]{1,0:T(8,128)(2,1)}, u32[]{:S(2)}) copy-start(bf16[256,256]{1,0:T(8,128)(2,1)} %param.18) | copy-start | bytes 393220
  94.4 3.1 %copy-start.9 = (f32[256]{0:T(256)S(1)}, f32[256]{0:T(256)}, u32[]{:S(2)}) copy-start(f32[256]{0:T(256)} %param.19) | copy-start | bytes 3076
  108.2 17.5 %all-to-all-start.6 = ((bf16[8,128,256]{2,1,0:T(8,128)(2,1)}), bf16[8,128,256]{2,1,0:T(8,128)(2,1)}, u32[]{:S(2)}, u32[]{:S(2)}) async-start(bf16[8,128,256]{2,1,0:T(8,128)(2,1)} %bitcast.56), calls=%async_computation.6 | async-start | bytes 1048576 | tf_op jit(solution)/shard_map/all_to_all | solution.py:92
  112.3 48.2 %all-reduce.3.cloned.1.call-start = ((), (), s32[]{:S(2)}) async-start(), calls=%async_computation.7 | async-start | bytes 524288 | tf_op jit(solution)/shard_map/psum | solution.py:106
  117.1 10.8 %copy-start.4 = (bf16[1024,256]{1,0:T(8,128)(2,1)S(1)}, bf16[1024,256]{1,0:T(8,128)(2,1)}, u32[]{:S(2)}) copy-start(bf16[1024,256]{1,0:T(8,128)(2,1)} %param.21) | copy-start | bytes 1572868
  125.7 34.9 %copy-start.6 = (bf16[256,256]{1,0:T(8,128)(2,1)S(1)}, bf16[256,256]{1,0:T(8,128)(2,1)}, u32[]{:S(2)}) copy-start(bf16[256,256]{1,0:T(8,128)(2,1)} %param.20) | copy-start | bytes 393220
  129.0 105.9 %all-reduce.5.cloned.1.call-start = ((), (), s32[]{:S(2)}) async-start(), calls=%async_computation.8 | async-start | bytes 524288 | tf_op jit(solution)/shard_map/psum | solution.py:106
Sparse Core Ops, SparseCore 0:
  129.1 31.3 all-reduce.2
  163.9 71.0 all-reduce.4
